TPU v7x, 32 devices: a whole 2x2x4 slice. The times are simulated.
32 devices in a mesh: seq: 8 (over y, x, core), head: 4 (over z).
Axes of the slice: x: 2, y: 2, z: 4, core: 2. Of those that a mesh axis runs over, the one named last changes fastest.
Arguments:
- mid: bfloat16 [2048, 3072], P('seq'), may hold values from -20 to 20
- second_in: bfloat16 [2048, 3072], P('seq'), may hold values from -20 to 20
- cotangent: bfloat16 [2048, 3072], P('seq'), may hold values from -6 to 6
- w_key: bfloat16 [3072, 1024], P(None, 'head'), may hold values from -0.109375 to 0.109375
- w_value: bfloat16 [3072, 1024], P(None, 'head'), may hold values from -0.109375 to 0.109375
- w_query: bfloat16 [2, 3072, 3072], P(None, None, 'head'), may hold values from -0.109375 to 0.109375
- w_out: bfloat16 [2, 3072, 3072], P(None, 'head'), may hold values from -0.109375 to 0.109375
- w_ret_out: bfloat16 [3072, 3072], P('head'), may hold values from -0.109375 to 0.109375
- ret_query: bfloat16 [2048, 3072], P('seq', 'head'), may hold values from -6 to 6
- ret_key: bfloat16 [2048, 3072], P('seq', 'head'), may hold values from -3 to 3
- ret_value: bfloat16 [2048, 3072], P('seq', 'head'), may hold values from -6 to 6
- gate: float32 [24, 2048], P('head', 'seq'), may hold values from 0 to 6
- decay_exp: int32 [24], P('head'), may hold values from 0 to 256
- mask_start: int32 [16], P('seq'), may hold values from 0 to 1920, as said below
Outputs:
- grad_mid: bfloat16 [2048, 3072], P('seq')
- grad_ret_query: bfloat16 [2048, 3072], P('seq', 'head')
- grad_ret_key: bfloat16 [2048, 3072], P('seq', 'head')
- grad_ret_value: bfloat16 [2048, 3072], P('seq', 'head')
- grad_w_key: float32 [3072, 1024], P(None, 'head')
- grad_w_value: float32 [3072, 1024], P(None, 'head')
Inputs may be any that keep to these rules, and one draw needn't show every extreme that they name: `mask_start`: the entry of each block of 128 queries is at most the position of that block's first query.
All inputs are finite; a program needn't handle non-finite values.
Results may differ from a plain program's by a relative error of at most 0.025.
The roundings to bfloat16 on the way count: a program that leaves them out, or rounds other values in their place, can miss the bound.
Values may be sent and summed in bfloat16 or wider, within the bound.
A program may use at most 192 MiB of HBM per device.

v0:
```python
import functools
import math

import jax
import jax.numpy as jnp
from jax import lax
from jax.experimental import pallas as pl
from jax.experimental.pallas import tpu as pltpu
from jax.sharding import PartitionSpec as P

E = 128
BLK = 128
RC = 128
F32 = jnp.float32
BF16 = jnp.bfloat16


def contract_last(left, right):
    return lax.dot_general(left, right, (((1,), (1,)), ((), ())), preferred_element_type=F32)


def contract_first(left, right):
    return lax.dot_general(left, right, (((0,), (0,)), ((), ())), preferred_element_type=F32)


def send(src, dst, send_sem, recv_sem, axis, index):
    return pltpu.make_async_remote_copy(
        src_ref=src,
        dst_ref=dst,
        send_sem=send_sem,
        recv_sem=recv_sem,
        device_id={axis: index},
        device_id_type=pl.DeviceIdType.MESH,
    )


class SeqPlace:
    def __init__(self):
        self.peers = lax.axis_size("seq")
        self.chips = self.peers // 2
        self.me = lax.axis_index("seq")
        self.chip = self.me // 2
        self.core = lax.rem(self.me, 2)
        self.sibling = self.me + 1 - 2 * self.core

    def mate(self, k):
        return lax.rem(self.me + 2 * k, self.peers)

    def mate_of_sibling(self, k):
        return lax.rem(self.sibling + 2 * k, self.peers)


def rows_at(ref, index, rows):
    return ref.at[pl.ds(pl.multiple_of(index * rows, rows), rows)]


class Gather:
    def __init__(self, place, source, out, sems):
        self.place, self.source, self.out = place, source, out
        self.sends, self.forwards, self.arrivals = sems
        self.rows = out.shape[0] // place.peers

    @staticmethod
    def semaphores(peers):
        return [
            pltpu.SemaphoreType.DMA((peers // 2,)),
            pltpu.SemaphoreType.DMA((peers // 2,)),
            pltpu.SemaphoreType.DMA((peers,)),
        ]

    def chunk(self, index):
        return rows_at(self.out, index, self.rows)

    def direct(self, k):
        p = self.place
        return send(self.source, self.chunk(p.me), self.sends.at[k], self.arrivals.at[p.me], "seq", p.mate(k))

    def relayed(self, k):
        p = self.place
        at = p.mate(k)
        src = self.source if k == 0 else self.chunk(at)
        return send(src, self.chunk(at), self.forwards.at[k], self.arrivals.at[at], "seq", p.sibling)

    def arrival(self, index):
        p = self.place
        return send(self.source, self.chunk(index), self.sends.at[0], self.arrivals.at[index], "seq", p.sibling)

    def start(self):
        for k in range(1, self.place.chips):
            self.direct(k).start()
        self.relayed(0).start()

    def relay(self):
        for k in range(1, self.place.chips):
            self.arrival(self.place.mate(k)).wait_recv()
            self.relayed(k).start()

    def finish(self):
        p = self.place
        for k in range(p.chips):
            self.arrival(p.mate_of_sibling(k)).wait_recv()
        for k in range(1, p.chips):
            self.direct(k).wait_send()
        for k in range(p.chips):
            self.relayed(k).wait_send()


class Scatter:
    def __init__(self, place, source, scratch):
        self.place, self.source = place, source
        self.from_sibling, self.summed, self.landed = scratch[:3]
        self.pair_send, self.pair_recv, self.far_send, self.far_recv = scratch[3:]
        self.rows = source.shape[0] // place.peers

    @staticmethod
    def scratch(peers, rows, columns):
        chips = peers // 2
        return [
            pltpu.VMEM((chips, rows, columns), BF16),
            pltpu.VMEM((chips, rows, columns), BF16),
            pltpu.VMEM((chips, rows, columns), BF16),
        ] + [pltpu.SemaphoreType.DMA((chips,))] * 4

    def pair(self, i):
        p = self.place
        return send(
            rows_at(self.source, 2 * i + 1 - p.core, self.rows),
            self.from_sibling.at[i],
            self.pair_send.at[i],
            self.pair_recv.at[i],
            "seq",
            p.sibling,
        )

    def far(self, k):
        p = self.place
        return send(
            self.summed.at[k], self.landed.at[k], self.far_send.at[k], self.far_recv.at[k], "seq", p.mate(k)
        )

    def pair_total(self, i):
        p = self.place
        self.pair(i).wait_recv()
        own = self.source[pl.ds(pl.multiple_of((2 * i + p.core) * self.rows, self.rows), self.rows), :]
        return own.astype(F32) + self.from_sibling[i].astype(F32)

    def start(self):
        for k in range(self.place.chips):
            self.pair(lax.rem(self.place.chip + 1 + k, self.place.chips)).start()

    def combine(self):
        p = self.place
        for k in range(1, p.chips):
            self.summed[k] = self.pair_total(lax.rem(p.chip + k, p.chips)).astype(BF16)
            self.far(k).start()

    def total(self):
        p = self.place
        total = self.pair_total(p.chip)
        for k in range(1, p.chips):
            self.far(k).wait_recv()
            total = total + self.landed[k].astype(F32)
        return total.astype(BF16)

    def finish(self):
        for i in range(self.place.chips):
            self.pair(i).wait_send()
        for k in range(1, self.place.chips):
            self.far(k).wait_send()


CHUNK = 16


class HeadSum:
    def __init__(self, part, residual, out, scratch):
        self.part, self.residual, self.out = part, residual, out
        self.landed, self.summed = scratch[:2]
        self.up_send, self.up_recv, self.back_send, self.back_recv = scratch[2:]
        self.n = lax.axis_size("head")
        self.z = lax.axis_index("head")
        self.count = part.shape[0] // CHUNK
        self.half = part.shape[1] // 2
        self.steps = self.count + 3 * (self.n - 1)

    @staticmethod
    def scratch(rows, columns):
        sems = pltpu.SemaphoreType.DMA((2, rows // CHUNK))
        return [pltpu.VMEM((rows, columns), BF16)] * 2 + [sems] * 4

    def piece(self, half, j):
        return pl.ds(pl.multiple_of(j * CHUNK, CHUNK), CHUNK), pl.ds(half * self.half, self.half)

    def way(self, half):
        if half == 0:
            return self.z, self.z - 1, self.z + 1
        return self.n - 1 - self.z, self.z + 1, self.z - 1

    def up(self, half, j):
        at = self.piece(half, j)
        return send(
            self.summed.at[at], self.landed.at[at], self.up_send.at[half, j], self.up_recv.at[half, j],
            "head", self.way(half)[2],
        )

    def back(self, half, j):
        at = self.piece(half, j)
        return send(
            self.out.at[at], self.out.at[at], self.back_send.at[half, j], self.back_recv.at[half, j],
            "head", self.way(half)[1],
        )

    def add(self, half, j):
        place = self.way(half)[0]
        at = self.piece(half, j)

        @pl.when(place == 0)
        def _():
            self.summed[at] = self.part[at]
            self.up(half, j).start()

        @pl.when(place > 0)
        def _():
            self.up(half, j).wait_recv()
            total = self.part[at].astype(F32) + self.landed[at].astype(F32)

            @pl.when(place < self.n - 1)
            def _():
                self.summed[at] = total.astype(BF16)
                self.up(half, j).start()

            @pl.when(place == self.n - 1)
            def _():
                self.out[at] = (self.residual[at].astype(F32) + total).astype(BF16)
                self.back(half, j).start()

    def give_back(self, half, j):
        place = self.way(half)[0]

        @pl.when(place < self.n - 1)
        def _():
            self.back(half, j).wait_recv()

            @pl.when(place > 0)
            def _():
                self.back(half, j).start()

    def run(self, first, last):
        def step(t, carry):
            @pl.when(t < self.count)
            def _():
                self.add(0, t)
                self.add(1, t)

            for half in (0, 1):
                j = t - 3 * (self.n - 1 - self.way(half)[0])

                @pl.when((j >= 0) & (j < self.count))
                def _(half=half, j=j):
                    self.give_back(half, j)

            return carry

        lax.fori_loop(first, last, step, 0)

    def finish(self):
        def step(j, carry):
            for half in (0, 1):
                place = self.way(half)[0]

                @pl.when(place < self.n - 1)
                def _(half=half):
                    self.up(half, j).wait_send()

                @pl.when(place > 0)
                def _(half=half):
                    self.back(half, j).wait_send()

            return carry

        lax.fori_loop(0, self.count, step, 0)


def meet(seq, head):
    barrier = pltpu.get_barrier_semaphore()
    expected = 0

    def greet(axis, index):
        pl.semaphore_signal(
            barrier, inc=1, device_id={axis: index}, device_id_type=pl.DeviceIdType.MESH
        )

    if seq is not None:
        for k in range(1, seq.chips):
            greet("seq", seq.mate(k))
        greet("seq", seq.sibling)
        expected = seq.chips
    if head:
        n, z = lax.axis_size("head"), lax.axis_index("head")

        @pl.when(z > 0)
        def _():
            greet("head", z - 1)

        @pl.when(z < n - 1)
        def _():
            greet("head", z + 1)

        expected = expected + jnp.where(z > 0, 1, 0) + jnp.where(z < n - 1, 1, 0)
    pl.semaphore_wait(barrier, expected)


def call(kernel, name, number, outs, scratch, *operands):
    whole = pl.BlockSpec(memory_space=pltpu.VMEM)
    return pl.pallas_call(
        kernel,
        out_shape=outs,
        in_specs=[whole] * len(operands),
        out_specs=jax.tree.map(lambda _: whole, outs),
        scratch_shapes=scratch,
        compiler_params=pltpu.CompilerParams(
            collective_id=number, has_side_effects=True, vmem_limit_bytes=56 * 2**20
        ),
        name=name,
    )(*operands)


def gather_kernel(x_ref, out_ref, *sems):
    place = SeqPlace()
    meet(place, False)
    gather = Gather(place, x_ref, out_ref, sems)
    gather.start()
    out_ref[pl.ds(pl.multiple_of(place.me * gather.rows, gather.rows), gather.rows), :] = x_ref[...]
    gather.relay()
    gather.finish()


def gather_seq(x, name, number):
    peers = lax.axis_size("seq")
    out = jax.ShapeDtypeStruct((peers * x.shape[0], x.shape[1]), x.dtype)
    return call(gather_kernel, name, number, out, Gather.semaphores(peers), x)


def scatter_kernel(x_ref, out_ref, *scratch):
    place = SeqPlace()
    meet(place, False)
    scatter = Scatter(place, x_ref, scratch)
    scatter.start()
    scatter.combine()
    out_ref[...] = scatter.total()
    scatter.finish()


def scatter_seq(x, name, number):
    peers = lax.axis_size("seq")
    rows = x.shape[0] // peers
    out = jax.ShapeDtypeStruct((rows, x.shape[1]), BF16)
    return call(scatter_kernel, name, number, out, Scatter.scratch(peers, rows, x.shape[1]), x)


def first_sum_kernel(part, residual, state, decay, out, states, decays, *scratch):
    place = SeqPlace()
    meet(place, True)
    head = HeadSum(part, residual, out, scratch[:6])
    small = Gather(place, decay, decays, scratch[6:9])
    large = Gather(place, state, states, scratch[9:12])
    small.start()
    large.start()
    head.run(0, head.count)
    for gather, source in ((small, decay), (large, state)):
        gather.out[pl.ds(pl.multiple_of(place.me * gather.rows, gather.rows), gather.rows), :] = source[...]
        gather.relay()
    head.run(head.count, head.steps)
    small.finish()
    large.finish()
    head.finish()


def first_sum(part, residual, state, decay):
    peers = lax.axis_size("seq")
    outs = (
        jax.ShapeDtypeStruct(part.shape, BF16),
        jax.ShapeDtypeStruct((peers * state.shape[0], state.shape[1]), state.dtype),
        jax.ShapeDtypeStruct((peers * decay.shape[0], decay.shape[1]), decay.dtype),
    )
    scratch = HeadSum.scratch(*part.shape) + Gather.semaphores(peers) + Gather.semaphores(peers)
    return call(first_sum_kernel, "first_sum", 1, outs, scratch, part, residual, state, decay)


def second_sum_kernel(part, residual, weights, out, totals, *scratch):
    place = SeqPlace()
    meet(place, True)
    head = HeadSum(part, residual, out, scratch[:6])
    scatter = Scatter(place, weights, scratch[6:13])
    own = rows_at(totals, place.me, totals.shape[0] // place.peers)
    gather = Gather(place, own, totals, scratch[13:16])
    scatter.start()
    head.run(0, 2)
    scatter.combine()
    head.run(2, 12)
    own[...] = scatter.total()
    gather.start()
    head.run(12, head.steps - 2)
    gather.relay()
    head.run(head.steps - 2, head.steps)
    gather.finish()
    scatter.finish()
    head.finish()


def second_sum(part, residual, weights):
    peers = lax.axis_size("seq")
    outs = (
        jax.ShapeDtypeStruct(part.shape, BF16),
        jax.ShapeDtypeStruct(weights.shape, BF16),
    )
    scratch = (
        HeadSum.scratch(*part.shape)
        + Scatter.scratch(peers, weights.shape[0] // peers, weights.shape[1])
        + Gather.semaphores(peers)
    )
    return call(second_sum_kernel, "second_sum", 3, outs, scratch, part, residual, weights)


def attention_kernel(group, step, has_prev, mask_ref, *refs):
    if has_prev:
        q_ref, g_ref, k_ref, v_ref, pk_ref, pv_ref, dq_ref, dk_ref, dv_ref = refs[:9]
        s_ref, dk_acc, dv_acc = refs[9:]
    else:
        q_ref, g_ref, k_ref, v_ref, dq_ref, dk_ref, dv_ref, s_ref = refs
        dk_acc, dv_acc = dk_ref, dv_ref
    factor = 1.0 / math.sqrt(E)
    block = pl.program_id(1)
    first_row = mask_ref[0] + block * BLK
    first_key = mask_ref[1 + block]
    rows = group * BLK

    @pl.when(block == 0)
    def _():
        if has_prev:
            dk_acc[...] = pk_ref[...]
            dv_acc[...] = pv_ref[...]
        else:
            dk_acc[...] = jnp.zeros_like(dk_acc)
            dv_acc[...] = jnp.zeros_like(dv_acc)

    q = jnp.concatenate([q_ref[:, i * E : (i + 1) * E] for i in range(group)], axis=0)
    g = jnp.concatenate([g_ref[:, i * E : (i + 1) * E] for i in range(group)], axis=0)
    low = first_key // step
    high = (first_row + BLK + step - 1) // step
    query_position = first_row + lax.broadcasted_iota(jnp.int32, (BLK, step), 0)

    def span(j):
        return pl.ds(pl.multiple_of(j * step, step), step)

    def score(j, top):
        scores = contract_last(q, k_ref[span(j), :]) * factor
        at = j * step + lax.broadcasted_iota(jnp.int32, (BLK, step), 1)
        seen = (at >= first_key) & (at <= query_position)
        seen = jnp.concatenate([seen] * group, axis=0)
        scores = jnp.where(seen, scores, -jnp.inf)
        s_ref[:, span(j)] = scores
        return jnp.maximum(top, jnp.max(scores, axis=-1, keepdims=True))

    top = lax.fori_loop(low, high, score, jnp.full((rows, 1), -jnp.inf, F32))

    def raise_(j, total):
        raised = jnp.exp(s_ref[:, span(j)] - top)
        s_ref[:, span(j)] = raised
        return total + jnp.sum(raised, axis=-1, keepdims=True)

    total = lax.fori_loop(low, high, raise_, jnp.zeros((rows, 1), F32))
    scale = 1.0 / total

    def output(j, out):
        probs = s_ref[:, span(j)] * scale
        s_ref[:, span(j)] = probs
        return out + jnp.dot(probs.astype(BF16), v_ref[span(j), :], preferred_element_type=F32)

    out = lax.fori_loop(low, high, output, jnp.zeros((rows, E), F32)).astype(BF16)
    delta = jnp.sum(g.astype(F32) * out.astype(F32), axis=-1, keepdims=True)

    def back(j, dq):
        probs = s_ref[:, span(j)]
        dprobs = contract_last(g, v_ref[span(j), :])
        dscores = (probs * (dprobs - delta) * factor).astype(BF16)
        dk_acc[span(j), :] += contract_first(dscores, q)
        dv_acc[span(j), :] += contract_first(probs.astype(BF16), g)
        return dq + jnp.dot(dscores, k_ref[span(j), :], preferred_element_type=F32)

    dq = lax.fori_loop(low, high, back, jnp.zeros((rows, E), F32)).astype(BF16)
    for i in range(group):
        dq_ref[:, i * E : (i + 1) * E] = dq[i * BLK : (i + 1) * BLK, :]
    if has_prev:

        @pl.when(block == pl.num_programs(1) - 1)
        def _():
            dk_ref[...] = dk_acc[...].astype(BF16)
            dv_ref[...] = dv_acc[...].astype(BF16)


def attention(mask, queries, grad_out, kv, previous):
    row_count, width = queries.shape
    key_count, both = kv.shape
    heads = both // (2 * E)
    group = width // (heads * E)
    step = 256 if key_count % 256 == 0 else BLK
    has_prev = previous is not None
    tile = pl.BlockSpec((BLK, group * E), lambda h, b, m: (b, h))
    key_block = pl.BlockSpec((key_count, E), lambda h, b, m: (0, h))
    value_block = pl.BlockSpec((key_count, E), lambda h, b, m: (0, h + heads))
    part = jax.ShapeDtypeStruct((key_count, heads * E), BF16 if has_prev else F32)
    scratch = [pltpu.VMEM((group * BLK, key_count), F32)]
    if has_prev:
        scratch += [pltpu.VMEM((key_count, E), F32)] * 2
    return pl.pallas_call(
        functools.partial(attention_kernel, group, step, has_prev),
        out_shape=(jax.ShapeDtypeStruct((row_count, width), BF16), part, part),
        grid_spec=pltpu.PrefetchScalarGridSpec(
            num_scalar_prefetch=1,
            grid=(heads, row_count // BLK),
            in_specs=[tile, tile, key_block, value_block] + [key_block] * (2 if has_prev else 0),
            out_specs=(tile, key_block, key_block),
            scratch_shapes=scratch,
        ),
        compiler_params=pltpu.CompilerParams(vmem_limit_bytes=48 * 2**20),
        cost_estimate=pl.CostEstimate(
            flops=10 * row_count * width * key_count, bytes_accessed=8 * 2**20, transcendentals=0
        ),
        name="attention_back",
    )(mask, queries, grad_out, kv, kv, *(previous or ()))


def retention_states(ret_key, ret_value, gate, decay_exp):
    length, width = ret_key.shape
    heads = gate.shape[0]
    size = width // heads
    count = length // RC
    key_blocks = ret_key.reshape(count, RC, heads, size)
    value_blocks = ret_value.reshape(count, RC, heads, size)
    rate = jnp.exp2(-decay_exp.astype(F32) / 64.0)
    accum = jnp.cumsum((-rate[:, None] * gate).reshape(heads, count, RC), axis=2)
    ends = accum[:, :, -1]
    shrink = jnp.transpose(jnp.exp(ends[:, :, None] - accum), (1, 2, 0))[..., None]
    weighted = (shrink * key_blocks).astype(BF16)
    own_state = jnp.einsum("csha,cshb->hcab", weighted, value_blocks, preferred_element_type=F32)
    return (accum, ends, shrink, own_state)


def grad_states(ret_query, grad_o, accum):
    heads, count, block = accum.shape
    size = ret_query.shape[1] // heads
    query_blocks = ret_query.reshape(count, block, heads, size)
    grad_blocks = grad_o.reshape(count, block, heads, size)
    grow = jnp.transpose(jnp.exp(accum), (1, 2, 0))[..., None]
    weighted = (grow * query_blocks).astype(BF16)
    own_grad = jnp.einsum("ctha,cthb->hcab", weighted, grad_blocks, preferred_element_type=F32) / E
    return (grow, own_grad)


def retention_grads(ret_query, ret_key, ret_value, grad_o, accum, shrink, grow, entering, after):
    length, width = ret_query.shape
    heads, count, block = accum.shape
    size = width // heads
    shape4 = (count, block, heads, size)
    query_blocks = ret_query.reshape(shape4)
    key_blocks = ret_key.reshape(shape4)
    value_blocks = ret_value.reshape(shape4)
    grad_blocks = grad_o.reshape(shape4)
    lower = jnp.arange(block)[:, None] >= jnp.arange(block)[None, :]
    diff = accum[:, :, :, None] - accum[:, :, None, :]
    weights = jnp.where(lower, jnp.exp(jnp.where(lower, diff, 0.0)), 0.0)
    dot = functools.partial(jnp.einsum, preferred_element_type=F32)
    first = (weights * dot("ctha,csha->hcts", grad_blocks, value_blocks)).astype(BF16)
    second = (weights * dot("ctha,csha->hcts", query_blocks, key_blocks)).astype(BF16)
    inner_query = dot("hcts,csha->ctha", first, key_blocks)
    inner_key = dot("hcts,ctha->csha", first, query_blocks)
    inner_value = dot("hcts,ctha->csha", second, grad_blocks)
    entering = entering.astype(BF16)
    after = after.astype(BF16)
    carried_query = dot("cthb,hcab->ctha", grad_blocks, entering)
    carried_key = dot("cshb,hcab->csha", value_blocks, after)
    carried_value = dot("csha,hcab->cshb", key_blocks, after)
    grad_query = ((inner_query + grow * carried_query) / E).astype(BF16).reshape(length, width)
    grad_key = (inner_key / E + shrink * carried_key).astype(BF16).reshape(length, width)
    grad_value = (inner_value / E + shrink * carried_value).astype(BF16).reshape(length, width)
    return (grad_query, grad_key, grad_value)


def local(
    mid,
    second_in,
    cotangent,
    w_key,
    w_value,
    w_query,
    w_out,
    w_ret_out,
    ret_query,
    ret_key,
    ret_value,
    gate,
    decay_exp,
    mask_start,
):
    row_count = mid.shape[0]
    peers, position = lax.axis_size("seq"), lax.axis_index("seq")
    accum, ends, shrink, own_state = retention_states(ret_key, ret_value, gate, decay_exp)
    decay_rows = jnp.exp(ends)
    heads, count = decay_rows.shape
    device_decay = jnp.prod(decay_rows, axis=1)
    device_state = jnp.zeros_like(own_state[:, 0])
    for block in range(count):
        device_state = decay_rows[:, block, None, None] * device_state + own_state[:, block]
    kv_own = jnp.concatenate(
        [
            jnp.dot(mid, w_key, preferred_element_type=F32).astype(BF16),
            jnp.dot(mid, w_value, preferred_element_type=F32).astype(BF16),
        ],
        axis=1,
    )
    kv = gather_seq(kv_own, "gather_kv", 0)
    mask = jnp.concatenate([(position * row_count)[None].astype(jnp.int32), mask_start])
    width = w_key.shape[1]

    queries = jnp.dot(second_in, w_query[1], preferred_element_type=F32).astype(BF16)
    grad_out = contract_last(cotangent, w_out[1]).astype(BF16)
    query_grad, upper_key, upper_value = attention(mask, queries, grad_out, kv, None)
    upstream, states, decays = first_sum(
        contract_last(query_grad, w_query[1]).astype(BF16),
        cotangent,
        device_state.astype(BF16).reshape(heads * E, E),
        jnp.pad(device_decay[None, :], ((0, 7), (0, E - heads))),
    )
    states = states.reshape(peers, heads, E, E)
    decays = decays.reshape(peers, 8, E)[:, 0, :heads]
    forward, backward = [], []
    for k in range(peers):
        pf = jnp.where(k < position, 1.0, 0.0) * jnp.ones((heads,), F32)
        pb = jnp.where(k > position, 1.0, 0.0) * jnp.ones((heads,), F32)
        for m in range(peers):
            if m > k:
                pf = pf * jnp.where(m < position, decays[m], 1.0)
            if m < k:
                pb = pb * jnp.where(m > position, decays[m], 1.0)
        forward.append(pf)
        backward.append(pb)
    incoming = sum(c[:, None, None] * states[k].astype(F32) for k, c in enumerate(forward))

    queries = jnp.dot(mid, w_query[0], preferred_element_type=F32).astype(BF16)
    grad_out = contract_last(upstream, w_out[0]).astype(BF16)
    query_grad, key_sum, value_sum = attention(
        mask, queries, grad_out, kv, (upper_key, upper_value)
    )
    kv_grad = scatter_seq(jnp.concatenate([key_sum, value_sum], axis=1), "scatter_kv", 2)
    w_kv = jnp.concatenate([w_key, w_value], axis=1)
    mid_part = contract_last(query_grad, w_query[0]) + contract_last(kv_grad, w_kv)
    grad_mid, weight_grad = second_sum(
        mid_part.astype(BF16), upstream, contract_first(mid, kv_grad).astype(BF16)
    )
    weight_grad = weight_grad.astype(F32)
    grad_w_key, grad_w_value = weight_grad[:, :width], weight_grad[:, width:]

    grad_o = contract_last(grad_mid, w_ret_out).astype(BF16)
    grow, own_grad = grad_states(ret_query, grad_o, accum)
    device_grad = jnp.zeros_like(device_state)
    for block in reversed(range(count)):
        device_grad = own_grad[:, block] + decay_rows[:, block, None, None] * device_grad
    grads = gather_seq(device_grad.astype(BF16).reshape(heads * E, E), "gather_grads", 4)
    grads = grads.reshape(peers, heads, E, E)
    outgoing = sum(c[:, None, None] * grads[k].astype(F32) for k, c in enumerate(backward))
    entering_list = []
    state_now = incoming
    for block in range(count):
        entering_list.append(state_now)
        state_now = decay_rows[:, block, None, None] * state_now + own_state[:, block]
    after_list = [state_now] * count
    state_now = outgoing
    for block in reversed(range(count)):
        after_list[block] = state_now
        state_now = own_grad[:, block] + decay_rows[:, block, None, None] * state_now
    entering = jnp.stack(entering_list, axis=1)
    after = jnp.stack(after_list, axis=1)
    grad_query, grad_key, grad_value = retention_grads(
        ret_query, ret_key, ret_value, grad_o, accum, shrink, grow, entering, after
    )
    return (grad_mid, grad_query, grad_key, grad_value, grad_w_key, grad_w_value)


def solution(mesh):
    placed = (
        P("seq", None),
        P("seq", None),
        P("seq", None),
        P(None, "head"),
        P(None, "head"),
        P(None, None, "head"),
        P(None, "head", None),
        P("head", None),
        P("seq", "head"),
        P("seq", "head"),
        P("seq", "head"),
        P("head", "seq"),
        P("head"),
        P("seq"),
    )
    return jax.shard_map(
        local,
        mesh=mesh,
        in_specs=placed,
        out_specs=(
            P("seq", None),
            P("seq", "head"),
            P("seq", "head"),
            P("seq", "head"),
            P(None, "head"),
            P(None, "head"),
        ),
        check_vma=False,
    )
```

profile of v0, /device:TPU:0, one launch (start us, length us, event | category | flops | bytes accessed | tf_op | source)
XLA Modules:
  0.0 864.8 jit_solution(10607162331997837429)
XLA Ops:
  0.7 0.8 pad_add_fusion.mask_ref
  2.2 0.8 broadcast_multiply_fusion
  3.0 1.8 reduce_window_sum.13
  7.1 0.7 broadcast_bitcast_fusion.1
  8.4 2.0 convolution_convert_fusion.3
  11.0 0.7 pad_maximum_fusion.3.x_ref
  11.8 3.8 fusion.43.refs_0_
  16.4 1.2 copy.68
  17.6 2.0 fusion.39
  20.0 1.2 copy.70
  21.8 4.4 fusion.46.refs_1_
  26.1 3.7 fusion.40.refs_0_
  30.6 1.0 fusion.70.state
  31.5 20.5 %gather_kv.1.refs_2_.refs_3_ = bf16[2048,512]{1,0:T(8,128)(2,1)} custom-call(bf16[256,512]{1,0:T(8,128)(2,1)} %pad_maximum_fusion.3.x_ref), custom_call_target="tpu_custom_call" | custom-call | tf_op jit(solution)/shard_map/gather_kv/pallas_call | solution.py:315
  52.0 8.8 %attention_back.2 = (bf16[256,768]{1,0:T(8,128)(2,1)S(1)}, f32[2048,256]{1,0:T(8,128)S(1)}, f32[2048,256]{1,0:T(8,128)S(1)}) custom-call(s32[3]{0:T(128)S(1)} %pad_add_fusion.mask_ref, bf16[256,768]{1,0:T(8,128)(2,1)S(1)} %fusion.43.refs_0_, bf16[256,768]{1,0:T(8,128)(2,1)S(1)} %fusion.46.refs_1_, bf16[2048,512]{1,0:T(8,128)(2,1)} %gather_kv.1.refs_2_.refs_3_, ...), custom_call_target="tpu_custom_call" | custom-call | flops 4026531840 | bytes 8388608 | tf_op jit(solution)/shard_map/attention_back/pallas_call | solution.py:516
  60.8 1.3 copy-done.2
  62.1 1.3 copy-done.3
  63.5 4.9 fusion.20.part
  68.4 352.9 %first_sum.1 = (bf16[256,3072]{1,0:T(8,128)(2,1)}, bf16[6144,128]{1,0:T(8,128)(2,1)}, f32[64,128]{1,0:T(8,128)}) custom-call(bf16[256,3072]{1,0:T(8,128)(2,1)} %fusion.20.part, bf16[256,3072]{1,0:T(8,128)(2,1)} %residual.1, bf16[768,128]{1,0:T(8,128)(2,1)} %fusion.70.state, f32[8,128]{1,0:T(8,128)} %pad.4.decay), custom_call_target="tpu_custom_call" | custom-call | tf_op jit(solution)/shard_map/first_sum/pallas_call | solution.py:315
  421.3 1.3 multiply_bitcast_fusion.12
  422.6 1.3 multiply_bitcast_fusion.11
  423.8 1.2 multiply_bitcast_fusion.10
  425.0 1.2 multiply_bitcast_fusion.9
  426.3 1.3 multiply_bitcast_fusion.8
  427.5 1.0 convert_multiply_fusion.15
  428.5 1.5 fusion.98
  430.0 1.1 fusion.94
  431.1 0.8 add_convert_fusion.1
  431.9 3.9 fusion.49.refs_1_
  435.9 9.7 %attention_back.3 = (bf16[256,768]{1,0:T(8,128)(2,1)S(1)}, bf16[2048,256]{1,0:T(8,128)(2,1)S(1)}, bf16[2048,256]{1,0:T(8,128)(2,1)S(1)}) custom-call(s32[3]{0:T(128)S(1)} %pad_add_fusion.mask_ref, bf16[256,768]{1,0:T(8,128)(2,1)S(1)} %fusion.40.refs_0_, bf16[256,768]{1,0:T(8,128)(2,1)S(1)} %fusion.49.refs_1_, bf16[2048,512]{1,0:T(8,128)(2,1)S(1)} %copy-done.1, ...), custom_call_target="tpu_custom_call" | custom-call | flops 4026531840 | bytes 8388608 | tf_op jit(solution)/shard_map/attention_back/pallas_call | solution.py:516
  445.6 1.5 pad_maximum_fusion.x_ref
  447.1 37.2 %scatter_kv.1 = bf16[256,512]{1,0:T(8,128)(2,1)} custom-call(bf16[2048,512]{1,0:T(8,128)(2,1)} %pad_maximum_fusion.x_ref), custom_call_target="tpu_custom_call" | custom-call | tf_op jit(solution)/shard_map/scatter_kv/pallas_call | solution.py:315
  484.3 3.9 fusion.8
  488.3 2.2 fusion.19.part
  490.4 2.7 fusion.18.weights
  493.1 334.0 %second_sum.1 = (bf16[256,3072]{1,0:T(8,128)(2,1)}, bf16[3072,512]{1,0:T(8,128)(2,1)}) custom-call(bf16[256,3072]{1,0:T(8,128)(2,1)} %fusion.19.part, bf16[256,3072]{1,0:T(8,128)(2,1)} %get-tuple-element.18.residual, bf16[3072,512]{1,0:T(8,128)(2,1)} %fusion.18.weights), custom_call_target="tpu_custom_call" | custom-call | tf_op jit(solution)/shard_map/second_sum/pallas_call | solution.py:315
  827.1 4.3 convolution_convert_fusion.1
  832.2 1.5 fusion.38
  833.6 1.3 convolution_multiply_fusion.2
  837.1 0.8 copy.178
  838.0 1.0 fusion.68.x_ref
  839.0 15.5 %gather_grads.1 = bf16[6144,128]{1,0:T(8,128)(2,1)} custom-call(bf16[768,128]{1,0:T(8,128)(2,1)} %fusion.68.x_ref), custom_call_target="tpu_custom_call" | custom-call | tf_op jit(solution)/shard_map/gather_grads/pallas_call | solution.py:315
  854.6 1.0 convert_multiply_fusion.14
  855.5 1.5 fusion.97
  858.6 0.8 copy.177
  859.7 0.8 copy.176
  860.5 3.2 fusion.96
  863.7 1.1 copy.180
  (103 shorter events, 11.4 us)
Async XLA Ops:
  0.6 7.7 copy-start
  4.8 6.1 copy-start.17
  5.0 5.9 copy-start.21
  5.0 5.9 copy-start.23
  5.7 4.6 copy-start.9
  10.4 1.4 copy-start.32
  11.8 3.8 copy-start.14
  21.7 8.1 copy-start.7
  29.9 0.7 copy-start.19
  29.9 0.7 copy-start.20
  60.8 1.3 copy-start.2
  62.1 1.3 copy-start.3
  428.5 2.6 copy-start.22
  430.0 1.9 copy-start.8
  431.9 3.9 copy-start.1
  484.3 3.9 copy-start.5
  484.3 3.9 copy-start.10
  484.3 3.9 copy-start.11
  832.1 2.8 copy-start.12
  832.1 2.8 copy-start.13
  832.1 2.8 copy-start.16
  835.4 1.0 copy-start.15
  836.9 1.1 copy-start.18
  854.5 2.5 copy-start.24
  854.5 2.5 copy-start.25
  854.5 2.5 copy-start.26
  854.5 2.5 copy-start.27
  854.5 2.5 copy-start.28
  854.5 2.5 copy-start.29
  854.5 2.5 copy-start.30
  854.5 2.5 copy-start.31
  858.3 2.2 copy-start.4
  860.5 3.2 copy-start.6
where the time goes:
time: 862 us; the launch traced here: 865 us
  Pallas kernels  779 us (90%)
  matrix products  43.8 us (5%)
  local copies, waits for them, and re-layouts  21.6 us (3%)
  other arithmetic  19.4 us (2%)
    pallas_call x5, Pallas kernels, call(): pl.pallas_call(kernel, out_shape=outs, in_specs=[whole] * len(operands),...  760 us
    dot_general x6, matrix products, contract_last(): lax.dot_general(left, right, (((1,), (1,)), ((), ())), preferred_element_...  23.5 us
    pallas_call x2, Pallas kernels, attention(): pl.pallas_call(functools.partial(attention_kernel, group, step, has_prev)...  18.5 us

commit v1 on v0

--- a/solution.py
+++ b/solution.py
@@ -170,6 +170,7 @@
 
 
 CHUNK = 16
+LAG = 2
 
 
 class HeadSum:
@@ -181,7 +182,7 @@
         self.z = lax.axis_index("head")
         self.count = part.shape[0] // CHUNK
         self.half = part.shape[1] // 2
-        self.steps = self.count + 3 * (self.n - 1)
+        self.steps = self.count + 2 * LAG * (self.n - 1)
 
     @staticmethod
     def scratch(rows, columns):
@@ -247,17 +248,18 @@
 
     def run(self, first, last):
         def step(t, carry):
-            @pl.when(t < self.count)
-            def _():
-                self.add(0, t)
-                self.add(1, t)
-
             for half in (0, 1):
-                j = t - 3 * (self.n - 1 - self.way(half)[0])
-
-                @pl.when((j >= 0) & (j < self.count))
-                def _(half=half, j=j):
-                    self.give_back(half, j)
+                place = self.way(half)[0]
+                up = t - LAG * place
+                down = t - LAG * (2 * (self.n - 1) - place)
+
+                @pl.when((up >= 0) & (up < self.count))
+                def _(half=half, up=up):
+                    self.add(half, up)
+
+                @pl.when((down >= 0) & (down < self.count))
+                def _(half=half, down=down):
+                    self.give_back(half, down)
 
             return carry
 

time: 862 us -> 308 us (0.36)
  Pallas kernels: 779 us -> 221 us
    pallas_call x5, Pallas kernels: 760 us -> 202 us  [call(): pl.pallas_call(kernel, out_shape=outs, in_specs=[whole] * len(operands),...]
where the time goes in v1:
time: 308 us; the launch traced here: 307 us
  Pallas kernels  221 us (72%)
  matrix products  43.8 us (14%)
  local copies, waits for them, and re-layouts  21.6 us (7%)
  other arithmetic  19.4 us (6%)
    pallas_call x5, Pallas kernels, call(): pl.pallas_call(kernel, out_shape=outs, in_specs=[whole] * len(operands),...  202 us
    dot_general x6, matrix products, contract_last(): lax.dot_general(left, right, (((1,), (1,)), ((), ())), preferred_element_...  23.5 us
    pallas_call x2, Pallas kernels, attention(): pl.pallas_call(functools.partial(attention_kernel, group, step, has_prev)...  18.5 us
    unnamed x76, local copies, waits for them, and re-layouts  10.1 us
    mul x5, other arithmetic, local(): pb = pb * jnp.where(m > position, decays[m], 1.0)  6.25 us

profile of v1, /device:TPU:0, one launch (start us, length us, event | category | flops | bytes accessed | tf_op | source)
XLA Modules:
  0.0 306.7 jit_solution(11437942850357803248)
XLA Ops:
  0.7 0.8 pad_add_fusion.mask_ref
  2.2 0.8 broadcast_multiply_fusion
  3.0 1.8 reduce_window_sum.13
  7.1 0.7 broadcast_bitcast_fusion.1
  8.4 2.0 convolution_convert_fusion.3
  11.0 0.7 pad_maximum_fusion.3.x_ref
  11.8 3.8 %fusion.43.refs_0_ = bf16[256,768]{1,0:T(8,128)(2,1)S(1)} fusion(bf16[256,3072]{1,0:T(8,128)(2,1)S(1)} %copy-done.32, bf16[2,3072,768]{2,1,0:T(8,128)(2,1)} %param.19), kind=kOutput, calls=%fused_computation.51 | convolution fusion | flops 1208156160 | bytes 6684672 | tf_op jit(solution)/shard_map/dot_general | solution.py:628
  16.4 1.2 copy.68
  17.6 2.0 fusion.39
  20.0 1.2 copy.70
  21.8 4.4 %fusion.46.refs_1_ = bf16[256,768]{1,0:T(8,128)(2,1)S(1)} fusion(bf16[256,3072]{1,0:T(8,128)(2,1)} %residual.1, bf16[2,768,3072]{2,1,0:T(8,128)(2,1)} %param.20), kind=kOutput, calls=%fused_computation.52 | convolution fusion | flops 1208156160 | bytes 6684672 | tf_op jit(solution)/shard_map/dot_general | solution.py:19
  26.1 3.7 %fusion.40.refs_0_ = bf16[256,768]{1,0:T(8,128)(2,1)S(1)} fusion(bf16[256,3072]{1,0:T(8,128)(2,1)S(1)} %copy-done, bf16[2,3072,768]{2,1,0:T(8,128)(2,1)} %param.19), kind=kOutput, calls=%fused_computation.50 | convolution fusion | flops 1208156160 | bytes 6684672 | tf_op jit(solution)/shard_map/dot_general | solution.py:652
  30.6 1.0 fusion.70.state
  31.5 20.5 %gather_kv.1.refs_2_.refs_3_ = bf16[2048,512]{1,0:T(8,128)(2,1)} custom-call(bf16[256,512]{1,0:T(8,128)(2,1)} %pad_maximum_fusion.3.x_ref), custom_call_target="tpu_custom_call" | custom-call | tf_op jit(solution)/shard_map/gather_kv/pallas_call | solution.py:317
  52.0 8.8 %attention_back.2 = (bf16[256,768]{1,0:T(8,128)(2,1)S(1)}, f32[2048,256]{1,0:T(8,128)S(1)}, f32[2048,256]{1,0:T(8,128)S(1)}) custom-call(s32[3]{0:T(128)S(1)} %pad_add_fusion.mask_ref, bf16[256,768]{1,0:T(8,128)(2,1)S(1)} %fusion.43.refs_0_, bf16[256,768]{1,0:T(8,128)(2,1)S(1)} %fusion.46.refs_1_, bf16[2048,512]{1,0:T(8,128)(2,1)} %gather_kv.1.refs_2_.refs_3_, ...), custom_call_target="tpu_custom_call" | custom-call | flops 4026531840 | bytes 8388608 | tf_op jit(solution)/shard_map/attention_back/pallas_call | solution.py:518
  60.8 1.3 copy-done.2
  62.1 1.3 copy-done.3
  63.5 4.9 %fusion.20.part = bf16[256,3072]{1,0:T(8,128)(2,1)} fusion(bf16[256,768]{1,0:T(8,128)(2,1)S(1)} %get-tuple-element.17, bf16[2,3072,768]{2,1,0:T(8,128)(2,1)} %param.19), kind=kOutput, calls=%fused_computation.22 | convolution fusion | flops 1208745984 | bytes 6684672 | tf_op jit(solution)/shard_map/dot_general | solution.py:19
  68.4 71.1 %first_sum.1 = (bf16[256,3072]{1,0:T(8,128)(2,1)}, bf16[6144,128]{1,0:T(8,128)(2,1)}, f32[64,128]{1,0:T(8,128)}) custom-call(bf16[256,3072]{1,0:T(8,128)(2,1)} %fusion.20.part, bf16[256,3072]{1,0:T(8,128)(2,1)} %residual.1, bf16[768,128]{1,0:T(8,128)(2,1)} %fusion.70.state, f32[8,128]{1,0:T(8,128)} %pad.4.decay), custom_call_target="tpu_custom_call" | custom-call | tf_op jit(solution)/shard_map/first_sum/pallas_call | solution.py:317
  139.5 1.3 multiply_bitcast_fusion.12
  140.8 1.3 multiply_bitcast_fusion.11
  142.0 1.2 multiply_bitcast_fusion.10
  143.2 1.2 multiply_bitcast_fusion.9
  144.5 1.3 multiply_bitcast_fusion.8
  145.8 1.0 convert_multiply_fusion.15
  146.7 1.5 fusion.98
  148.2 1.1 fusion.94
  149.3 0.8 add_convert_fusion.1
  150.1 3.9 %fusion.49.refs_1_ = bf16[256,768]{1,0:T(8,128)(2,1)S(1)} fusion(bf16[256,3072]{1,0:T(8,128)(2,1)S(1)} %copy-done.8, bf16[2,768,3072]{2,1,0:T(8,128)(2,1)} %param.20), kind=kOutput, calls=%fused_computation.53 | convolution fusion | flops 1208156160 | bytes 6684672 | tf_op jit(solution)/shard_map/dot_general | solution.py:19
  154.1 9.7 %attention_back.3 = (bf16[256,768]{1,0:T(8,128)(2,1)S(1)}, bf16[2048,256]{1,0:T(8,128)(2,1)S(1)}, bf16[2048,256]{1,0:T(8,128)(2,1)S(1)}) custom-call(s32[3]{0:T(128)S(1)} %pad_add_fusion.mask_ref, bf16[256,768]{1,0:T(8,128)(2,1)S(1)} %fusion.40.refs_0_, bf16[256,768]{1,0:T(8,128)(2,1)S(1)} %fusion.49.refs_1_, bf16[2048,512]{1,0:T(8,128)(2,1)S(1)} %copy-done.1, ...), custom_call_target="tpu_custom_call" | custom-call | flops 4026531840 | bytes 8388608 | tf_op jit(solution)/shard_map/attention_back/pallas_call | solution.py:518
  163.8 1.5 pad_maximum_fusion.x_ref
  165.3 38.3 %scatter_kv.1 = bf16[256,512]{1,0:T(8,128)(2,1)} custom-call(bf16[2048,512]{1,0:T(8,128)(2,1)} %pad_maximum_fusion.x_ref), custom_call_target="tpu_custom_call" | custom-call | tf_op jit(solution)/shard_map/scatter_kv/pallas_call | solution.py:317
  203.6 3.9 %fusion.8 = f32[256,3072]{1,0:T(8,128)S(1)} fusion(bf16[256,768]{1,0:T(8,128)(2,1)S(1)} %get-tuple-element.21, bf16[2,3072,768]{2,1,0:T(8,128)(2,1)} %param.19), kind=kOutput, calls=%fused_computation.8 | convolution fusion | flops 1207959552 | bytes 8257536 | tf_op jit(solution)/shard_map/dot_general | solution.py:19
  207.6 2.2 fusion.19.part
  209.8 2.7 fusion.18.weights
  212.4 58.0 %second_sum.1 = (bf16[256,3072]{1,0:T(8,128)(2,1)}, bf16[3072,512]{1,0:T(8,128)(2,1)}) custom-call(bf16[256,3072]{1,0:T(8,128)(2,1)} %fusion.19.part, bf16[256,3072]{1,0:T(8,128)(2,1)} %get-tuple-element.18.residual, bf16[3072,512]{1,0:T(8,128)(2,1)} %fusion.18.weights), custom_call_target="tpu_custom_call" | custom-call | tf_op jit(solution)/shard_map/second_sum/pallas_call | solution.py:317
  270.4 4.3 %convolution_convert_fusion.1 = bf16[256,768]{1,0:T(8,128)(2,1)S(1)} fusion(bf16[256,3072]{1,0:T(8,128)(2,1)} %get-tuple-element.107, bf16[768,3072]{1,0:T(8,128)(2,1)} %param.21), kind=kOutput, calls=%fused_computation.54 | convolution fusion | flops 1208156160 | bytes 6684672 | tf_op jit(solution)/shard_map/dot_general | solution.py:19
  275.5 1.5 fusion.38
  277.0 1.3 convolution_multiply_fusion.2
  280.5 0.8 copy.178
  281.3 1.0 fusion.68.x_ref
  282.3 14.1 %gather_grads.1 = bf16[6144,128]{1,0:T(8,128)(2,1)} custom-call(bf16[768,128]{1,0:T(8,128)(2,1)} %fusion.68.x_ref), custom_call_target="tpu_custom_call" | custom-call | tf_op jit(solution)/shard_map/gather_grads/pallas_call | solution.py:317
  296.5 1.0 convert_multiply_fusion.14
  297.5 1.5 fusion.97
  300.5 0.8 copy.177
  301.6 0.8 copy.176
  302.4 3.2 %fusion.96 = (f32[3072,256]{1,0:T(8,128)}, f32[3072,256]{1,0:T(8,128)}) fusion(bf16[3072,512]{1,0:T(8,128)(2,1)S(1)} %copy-done.4), kind=kLoop, calls=%fused_computation.171 | loop fusion | bytes 12582912 | tf_op jit(solution)/shard_map/slice | solution.py:664
  305.6 1.1 copy.180
  (103 shorter events, 11.4 us)
Async XLA Ops:
  0.6 7.7 %copy-start = (bf16[256,3072]{1,0:T(8,128)(2,1)S(1)}, bf16[256,3072]{1,0:T(8,128)(2,1)}, u32[]{:S(2)}) copy-start(bf16[256,3072]{1,0:T(8,128)(2,1)} %param.14) | copy-start | bytes 4718596
  4.8 6.1 %copy-start.17 = (f32[6,2,128]{2,1,0:T(2,128)}, f32[6,2,128]{2,1,0:T(2,128)S(1)}, u32[]{:S(2)}) copy-start(f32[6,2,128]{2,1,0:T(2,128)S(1)} %reduce_window_sum.13) | copy-start | bytes 18436
  5.0 5.9 %copy-start.21 = (f32[6]{0:T(128)}, f32[6]{0:T(128)S(1)}, u32[]{:S(2)}) copy-start(f32[6]{0:T(128)S(1)} %get-tuple-element.89) | copy-start | bytes 76
  5.0 5.9 %copy-start.23 = (f32[6]{0:T(128)}, f32[6]{0:T(128)S(1)}, u32[]{:S(2)}) copy-start(f32[6]{0:T(128)S(1)} %get-tuple-element.90) | copy-start | bytes 76
  5.7 4.6 %copy-start.9 = (bf16[3072,256]{1,0:T(8,128)(2,1)S(1)}, bf16[3072,256]{1,0:T(8,128)(2,1)}, u32[]{:S(2)}) copy-start(bf16[3072,256]{1,0:T(8,128)(2,1)} %param.18) | copy-start | bytes 4718596
  10.4 1.4 copy-start.32
  11.8 3.8 %copy-start.14 = (bf16[256,768]{1,0:T(8,128)(2,1)S(1)}, bf16[256,768]{1,0:T(8,128)(2,1)}, u32[]{:S(2)}) copy-start(bf16[256,768]{1,0:T(8,128)(2,1)} %param.22) | copy-start | bytes 1179652
  21.7 8.1 %copy-start.7 = (bf16[2,128,6,128]{3,1,0,2:T(8,128)(2,1)}, bf16[2,128,6,128]{3,1,0,2:T(8,128)(2,1)S(1)}, u32[]{:S(2)}) copy-start(bf16[2,128,6,128]{3,1,0,2:T(8,128)(2,1)S(1)} %copy.72) | copy-start | bytes 1179652
  29.9 0.7 copy-start.19
  29.9 0.7 copy-start.20
  60.8 1.3 copy-start.2
  62.1 1.3 copy-start.3
  146.7 2.6 copy-start.22
  148.2 1.9 copy-start.8
  150.1 3.9 %copy-start.1 = (bf16[2048,512]{1,0:T(8,128)(2,1)S(1)}, bf16[2048,512]{1,0:T(8,128)(2,1)}, u32[]{:S(2)}) copy-start(bf16[2048,512]{1,0:T(8,128)(2,1)} %gather_kv.1.refs_2_.refs_3_) | copy-start | bytes 6291460
  203.6 3.9 %copy-start.5 = (bf16[256,512]{1,0:T(8,128)(2,1)S(1)}, bf16[256,512]{1,0:T(8,128)(2,1)}, u32[]{:S(2)}) copy-start(bf16[256,512]{1,0:T(8,128)(2,1)} %scatter_kv.1) | copy-start | bytes 786436
  203.6 3.9 %copy-start.10 = (bf16[3072,256]{1,0:T(8,128)(2,1)S(1)}, bf16[3072,256]{1,0:T(8,128)(2,1)}, u32[]{:S(2)}) copy-start(bf16[3072,256]{1,0:T(8,128)(2,1)} %param.18) | copy-start | bytes 4718596
  203.6 3.9 %copy-start.11 = (bf16[3072,256]{1,0:T(8,128)(2,1)S(1)}, bf16[3072,256]{1,0:T(8,128)(2,1)}, u32[]{:S(2)}) copy-start(bf16[3072,256]{1,0:T(8,128)(2,1)} %param.17) | copy-start | bytes 4718596
  275.4 2.8 copy-start.12
  275.5 2.8 copy-start.13
  275.5 2.8 copy-start.16
  278.7 1.0 copy-start.15
  280.2 1.1 copy-start.18
  296.4 2.5 copy-start.24
  296.4 2.5 copy-start.25
  296.4 2.5 copy-start.26
  296.5 2.5 copy-start.27
  296.5 2.5 copy-start.28
  296.5 2.5 copy-start.29
  296.5 2.5 copy-start.30
  296.5 2.5 copy-start.31
  300.2 2.2 copy-start.4
  302.4 3.2 %copy-start.6 = (bf16[256,3072]{1,0:T(8,128)(2,1)S(1)}, bf16[256,3072]{1,0:T(8,128)(2,1)}, u32[]{:S(2)}) copy-start(bf16[256,3072]{1,0:T(8,128)(2,1)} %get-tuple-element.107) | copy-start | bytes 4718596
